TPU v7x, 256 devices: a whole 4x4x8 slice. The times are simulated.
256 devices in a mesh: fsdp: 32 (over x_hi, z, core), tp: 8 (over x_lo, y).
Axes of the slice: x: 4 (x_hi: 2, x_lo: 2; x = x_hi * 2 + x_lo), y: 4, z: 8, core: 2. Of those that a mesh axis runs over, the one named last changes fastest.
Arguments:
- tokens: bfloat16 [4096, 3584], P('fsdp', 'tp'), may hold values from -6 to 6
- norm_gain: bfloat16 [3584], replicated, may hold values from 0.5 to 1.5
- gate_weight: bfloat16 [3584, 10240], P('fsdp', 'tp'), may hold values from -0.09375 to 0.09375
- up_weight: bfloat16 [3584, 10240], P('fsdp', 'tp'), may hold values from -0.09375 to 0.09375
- down_weight: bfloat16 [3584, 10240], P('fsdp', 'tp'), may hold values from -0.0625 to 0.0625
- probes: bfloat16 [2, 3584, 10240], P(None, 'fsdp', 'tp'), may hold values from -0.0625 to 0.0625
Outputs:
- layer_out: bfloat16 [4096, 3584], P('tp', 'fsdp')
- token_curv: float32 [4096], P('tp')
All inputs are finite; a program needn't handle non-finite values.
Results may differ from a plain program's by a relative error of at most 0.014.
Values may be sent and summed in bfloat16 or wider, within the bound.
No kernel may reach another device: no remote copies, remote signals or barrier semaphores. Data moves between devices by JAX's collectives and lax.ppermute only.
A program may use at most 64 MiB of HBM per device.

v0:
```python
import jax
import jax.numpy as jnp
from jax import lax
from jax.sharding import PartitionSpec as P

D = 3584
PROBES = 2


epsilon = 1e-06


def in_order(blocks, dim):
    blocks = jnp.moveaxis(blocks, 0, dim)
    dims = blocks.shape
    return blocks.reshape(*dims[:dim], dims[dim] * dims[dim + 1], *dims[dim + 2 :])


def sent_to_all(array, axis):
    peers = lax.axis_size(axis)
    return lax.all_to_all(
        jnp.broadcast_to(array[None], (peers, *array.shape)), axis, 0, 0, tiled=True
    )


def gathered_copies(array, axis, dim):
    return in_order(sent_to_all(array, axis), dim)


def sent_together(arrays, axis, dim, along):
    ends, at = ([], 0)
    for a in arrays[:-1]:
        at += a.shape[along]
        ends.append(at)
    both = jnp.concatenate(arrays, axis=along)
    return tuple(jnp.split(lax.all_gather(both, axis, axis=dim, tiled=True), ends, axis=along))


def in_blocks(array, dim, peers):
    dims = array.shape
    blocks = array.reshape(*dims[:dim], peers, dims[dim] // peers, *dims[dim + 1 :])
    return jnp.moveaxis(blocks, dim, 0)


def summed_on_arrival(array, axis, dim):
    peers = lax.axis_size(axis)
    blocks = lax.all_to_all(in_blocks(array, dim, peers), axis, 0, 0, tiled=True)
    return jnp.sum(blocks.astype(jnp.float32), axis=0)


def of_everyone(array, axis):
    return sent_to_all(array, axis).sum(axis=0)


def on_device(tokens, norm_gain, gate_weight, up_weight, down_weight, probes):
    features = gathered_copies(tokens, "tp", 1)
    widened = features.astype(jnp.float32)
    inverse_rms = lax.rsqrt(jnp.mean(widened * widened, axis=1, keepdims=True) + epsilon)
    normed = (widened * inverse_rms * norm_gain.astype(jnp.float32)).astype(jnp.bfloat16)
    gate_full, up_full = sent_together((gate_weight, up_weight), "fsdp", 0, 1)
    gate_sum = jnp.dot(normed, gate_full, preferred_element_type=jnp.float32)
    up_sum = jnp.dot(normed, up_full, preferred_element_type=jnp.float32)
    hidden = (jax.nn.silu(gate_sum) * up_sum).astype(jnp.bfloat16)
    stacked = jnp.concatenate([down_weight[None], probes], axis=0)
    count = stacked.shape[0]
    col_width = stacked.shape[1]
    flat_weights = stacked.reshape(count * col_width, stacked.shape[2])
    partial_terms = lax.dot_general(
        lax.all_gather(hidden, "fsdp", axis=0, tiled=True),
        flat_weights,
        (((1,), (1,)), ((), ())),
        preferred_element_type=jnp.float32,
    )
    summed = summed_on_arrival(partial_terms.astype(jnp.bfloat16), "tp", 0)
    summed_parts = summed.reshape(summed.shape[0], count, col_width)
    primal = summed_parts[:, 0, :]
    tangents = summed_parts[:, 1:, :]
    squashed = jax.nn.sigmoid(primal)
    slope = squashed * (1.0 - squashed)
    tangent_sq = jnp.sum(tangents * tangents, axis=1)
    local_curv = jnp.sum(slope * tangent_sq, axis=1) / (PROBES * D)
    token_curv = of_everyone(local_curv, "fsdp")
    return (primal.astype(jnp.bfloat16), token_curv)


def solution(mesh):
    return jax.shard_map(
        on_device,
        mesh=mesh,
        in_specs=(
            P("fsdp", "tp"),
            P(),
            P("fsdp", "tp"),
            P("fsdp", "tp"),
            P("fsdp", "tp"),
            P(None, "fsdp", "tp"),
        ),
        out_specs=(P("tp", "fsdp"), P("tp")),
        check_vma=False,
    )
```

profile of v0, /device:TPU:1, one launch (start us, length us, event | category | flops | bytes accessed | tf_op | source)
XLA Modules:
  0.0 352.6 jit_solution(11822923586931489641)
XLA Ops:
  7.2 0.0 all-gather.3.cloned.1.call-start
  7.2 1.9 pad_maximum_fusion.1
  9.1 0.0 all-gather.3.cloned.1.call-update
  9.1 1.9 broadcast_in_dim.6
  11.1 5.9 %all-to-all-start = ((bf16[8,128,448]{1,2,0:T(8,128)(2,1)}), bf16[8,128,448]{1,2,0:T(8,128)(2,1)S(1)}, u32[]{:S(2)}, u32[]{:S(2)}) async-start(bf16[8,128,448]{1,2,0:T(8,128)(2,1)} %broadcast_in_dim.6), calls=%async_computation | async-start | bytes 1835008 | tf_op jit(solution)/shard_map/all_to_all | solution.py:21
  17.0 0.0 all-gather.5.cloned.1.call-start
  17.1 0.7 convert_element_type.38
  17.8 12.6 %all-to-all-done = bf16[8,128,448]{1,2,0:T(8,128)(2,1)S(1)} async-done(((bf16[8,128,448]{1,2,0:T(8,128)(2,1)}), bf16[8,128,448]{1,2,0:T(8,128)(2,1)S(1)}, u32[]{:S(2)}, u32[]{:S(2)}) %all-to-all-start) | async-done | bytes 917536 | tf_op jit(solution)/shard_map/all_to_all | solution.py:21
  30.3 0.5 multiply_reduce_fusion
  30.8 0.5 fusion.11
  31.4 130.5 %all-gather.3.cloned.1.call-done = bf16[3584,2560]{1,0:T(8,128)(2,1)} async-done(((bf16[112,2560]{1,0:T(8,128)(2,1)}), bf16[3584,2560]{1,0:T(8,128)(2,1)}) %all-gather.3.cloned.1.call-update) | async-done | bytes 18350096 | tf_op jit(solution)/shard_map/all_gather | solution.py:36
  161.8 5.1 %fusion.2 = f32[128,1280]{1,0:T(8,128)S(1)} fusion(bf16[128,3584]{0,1:T(8,128)(2,1)S(1)} %fusion.11, bf16[3584,2560]{1,0:T(8,128)(2,1)} %all-gather.3.cloned.1.call-done), kind=kOutput, calls=%fused_computation.2 | convolution fusion | flops 1174405120 | bytes 10747904 | tf_op jit(solution)/shard_map/dot_general | solution.py:61
  167.0 0.0 copy-start
  167.0 0.0 copy-start.1
  167.0 5.9 %fusion.7 = bf16[128,1280]{1,0:T(8,128)(2,1)} fusion(bf16[128,3584]{0,1:T(8,128)(2,1)S(1)} %fusion.11, bf16[3584,2560]{1,0:T(8,128)(2,1)} %all-gather.3.cloned.1.call-done, f32[128,1280]{1,0:T(8,128)S(1)} %fusion.2), kind=kOutput, calls=%fused_computation.8 | convolution fusion | flops 1175388160 | bytes 11075584 | tf_op jit(solution)/shard_map/dot_general | solution.py:62
  172.8 0.0 all-gather.5.cloned.1.call-update
  172.9 0.0 copy-done
  172.9 0.0 copy-done.1
  172.9 0.1 pad_maximum_fusion
  173.0 105.2 %all-gather.5.cloned.1.call-done = bf16[4096,1280]{1,0:T(8,128)(2,1)} async-done(((bf16[128,1280]{1,0:T(8,128)(2,1)}), bf16[4096,1280]{1,0:T(8,128)(2,1)}) %all-gather.5.cloned.1.call-update) | async-done | bytes 10485776 | tf_op jit(solution)/shard_map/all_gather | solution.py:69
  278.1 11.1 %convolution_convert_fusion = bf16[4096,336]{0,1:T(8,128)(2,1)S(1)} fusion(bf16[4096,1280]{1,0:T(8,128)(2,1)} %all-gather.5.cloned.1.call-done, bf16[336,1280]{1,0:T(8,128)(2,1)S(1)} %bitcast.28), kind=kOutput, calls=%fused_computation.5 | convolution fusion | flops 3524591616 | bytes 14098432 | tf_op jit(solution)/shard_map/dot_general | solution.py:68
  289.2 0.3 copy.16
  289.5 37.0 %all_to_all.16 = bf16[8,512,336]{1,2,0:T(8,128)(2,1)S(1)} all-to-all(bf16[8,512,336]{1,2,0:T(8,128)(2,1)S(1)} %bitcast.23), channel_id=1, replica_groups=mesh['fsdp'=32,'tp'=8] {'tp'}, dimensions={0} | all-to-all | bytes 5505024 | tf_op jit(solution)/shard_map/all_to_all | solution.py:47
  326.4 0.4 convert_reduce_fusion
  326.9 0.1 fusion.14
  327.0 0.7 broadcast_in_dim.8
  327.6 7.9 %all-to-all-start.2 = ((f32[32,1,512]{2,1,0:T(1,128)}), f32[32,1,512]{2,1,0:T(1,128)S(1)}, u32[]{:S(2)}, u32[]{:S(2)}) async-start(f32[32,1,512]{2,1,0:T(1,128)} %broadcast_in_dim.8), calls=%async_computation.2 | async-start | bytes 131072 | tf_op jit(solution)/shard_map/all_to_all | solution.py:21
  335.5 0.7 fusion.15
  336.2 8.9 %all-to-all-done.2 = f32[32,1,512]{2,1,0:T(1,128)S(1)} async-done(((f32[32,1,512]{2,1,0:T(1,128)}), f32[32,1,512]{2,1,0:T(1,128)S(1)}, u32[]{:S(2)}, u32[]{:S(2)}) %all-to-all-start.2) | async-done | bytes 65568 | tf_op jit(solution)/shard_map/all_to_all | solution.py:21
  345.1 0.6 reduce_sum.49
  (3 shorter events, 0.1 us)
Async XLA Ops:
  7.2 154.7 %all-gather.3.cloned.1.call-start = ((), (), s32[]{:S(2)}) async-start(), calls=%async_computation.3 | async-start | bytes 18923520 | tf_op jit(solution)/shard_map/all_gather | solution.py:36
  11.1 19.2 %all-to-all-start = ((bf16[8,128,448]{1,2,0:T(8,128)(2,1)}), bf16[8,128,448]{1,2,0:T(8,128)(2,1)S(1)}, u32[]{:S(2)}, u32[]{:S(2)}) async-start(bf16[8,128,448]{1,2,0:T(8,128)(2,1)} %broadcast_in_dim.6), calls=%async_computation | async-start | bytes 1835008 | tf_op jit(solution)/shard_map/all_to_all | solution.py:21
  17.0 261.1 %all-gather.5.cloned.1.call-start = ((), (), s32[]{:S(2)}) async-start(), calls=%async_computation.4 | async-start | bytes 10813440 | tf_op jit(solution)/shard_map/all_gather | solution.py:69
  167.0 5.9 %copy-start = (bf16[2,112,1280]{2,1,0:T(8,128)(2,1)S(1)}, bf16[2,112,1280]{2,1,0:T(8,128)(2,1)}, u32[]{:S(2)}) copy-start(bf16[2,112,1280]{2,1,0:T(8,128)(2,1)} %param.11) | copy-start | bytes 1720324
  167.0 5.9 %copy-start.1 = (bf16[112,1280]{1,0:T(8,128)(2,1)S(1)}, bf16[112,1280]{1,0:T(8,128)(2,1)}, u32[]{:S(2)}) copy-start(bf16[112,1280]{1,0:T(8,128)(2,1)} %param.10) | copy-start | bytes 860164
  327.6 17.5 %all-to-all-start.2 = ((f32[32,1,512]{2,1,0:T(1,128)}), f32[32,1,512]{2,1,0:T(1,128)S(1)}, u32[]{:S(2)}, u32[]{:S(2)}) async-start(f32[32,1,512]{2,1,0:T(1,128)} %broadcast_in_dim.8), calls=%async_computation.2 | async-start | bytes 131072 | tf_op jit(solution)/shard_map/all_to_all | solution.py:21
Sparse Core Ops, SparseCore 0:
  10.7 151.0 all-gather.2
  173.0 105.1 all-gather.4
where the time goes:
time: 353 us
  waiting for transfers between devices  257 us (73%)
  blocking collectives  37 us (10%)
  matrix products  22 us (6%)
  between operations  14.1 us (4%)
  starting transfers between devices  13.9 us (4%)
  other arithmetic  4.9 us (1%)
    all_gather x1, waiting for transfers between devices, sent_together(): lax.all_gather(both, axis, axis=dim, tiled=True)  130 us
    all_gather x1, waiting for transfers between devices, on_device(): lax.all_gather(hidden, 'fsdp', axis=0, tiled=True)  105 us
    all_to_all x1, blocking collectives, summed_on_arrival(): lax.all_to_all(in_blocks(array, dim, peers), axis, 0, 0, tiled=True)  37 us
    all_to_all x2, waiting for transfers between devices, sent_to_all(): lax.all_to_all(jnp.broadcast_to(array[None], (peers, *array.shape)), axis...  21.5 us
    all_to_all x2, starting transfers between devices, sent_to_all(): lax.all_to_all(jnp.broadcast_to(array[None], (peers, *array.shape)), axis...  13.8 us
    dot_general x1, matrix products, on_device(): lax.dot_general(lax.all_gather(hidden, 'fsdp', axis=0, tiled=True), flat_...  11.1 us
  transfers between devices with their start and end apart: 4, of which 4 were waited for; matrix products, arithmetic and copies ran while one was open for 1% of the time, Pallas kernels for 0%

commit v1 on v0

v1 whole, which is shorter than its diff:
```python
import jax
import jax.numpy as jnp
from jax import lax
from jax.sharding import Mesh
from jax.sharding import PartitionSpec as P

D = 3584
PROBES = 2
AXES = {"xh": 2, "z": 8, "c": 2, "xl": 2, "y": 4}

epsilon = 1e-06


def moved(array, axes, shift):
    n = lax.axis_size(axes)
    return lax.ppermute(array, axes, [(i, (i + shift) % n) for i in range(n)])


def in_order_of(axis, own, other):
    first = lax.axis_index(axis) == 0
    return jnp.stack([jnp.where(first, own, other), jnp.where(first, other, own)])


def on_device(tokens, norm_gain, gate_weight, up_weight, down_weight, probes):
    rows, units = gate_weight.shape
    part = units // 4

    halves = [w.reshape(rows, 4, part).transpose(1, 0, 2) for w in (gate_weight, up_weight)]
    sent = jnp.concatenate(halves, axis=2)
    got = lax.all_to_all(sent, ("xh", "c"), 0, 0, tiled=True)
    gathered = lax.all_gather(got, "z", axis=0)
    weights = gathered.reshape(8, 2, 2, rows, 2 * part).transpose(1, 0, 2, 3, 4)
    weights = weights.reshape(D, 2 * part)

    block, width = tokens.shape
    spread = jnp.broadcast_to(tokens[None], (8, block, width))
    features = lax.all_to_all(spread, ("xl", "y"), 0, 0, tiled=True)
    features = jnp.moveaxis(features, 0, 1).reshape(block, D)
    widened = features.astype(jnp.float32)
    inverse_rms = lax.rsqrt(jnp.mean(widened * widened, axis=1, keepdims=True) + epsilon)
    own = (widened * inverse_rms * norm_gain.astype(jnp.float32)).astype(jnp.bfloat16)
    pair = in_order_of("xh", own, moved(own, "xh", 1))
    quad = in_order_of("c", pair, moved(pair, "c", 1))
    normed = quad.transpose(1, 0, 2, 3).reshape(4 * block, D)

    sums = jnp.dot(normed, weights, preferred_element_type=jnp.float32)
    gate_sum, up_sum = sums[:, :part], sums[:, part:]
    hidden = (jax.nn.silu(gate_sum) * up_sum).astype(jnp.bfloat16)

    stacked = jnp.concatenate([down_weight[None], probes], axis=0)
    count = stacked.shape[0]
    flat = stacked.reshape(count * rows, units)
    xs = ("xh", "xl")
    ring = [flat] + [moved(flat, xs, s) for s in (1, 2, 3)]
    x = lax.axis_index("xh") * 2 + lax.axis_index("xl")
    ring = jnp.stack(ring)
    by_x = jnp.stack([ring[(x - i) % 4] for i in range(4)])
    by_c = in_order_of("c", by_x, moved(by_x, "c", 1))
    matrices = by_c.reshape(2, 2, 2, count * rows, units).transpose(1, 0, 3, 2, 4)
    matrices = matrices.reshape(4 * count * rows, 2 * units)

    chunks = hidden.reshape(2, 2, 2, block // 2, part).transpose(1, 0, 2, 3, 4)
    chunks = chunks.reshape(8, block // 2, part)
    mine = lax.all_to_all(chunks, ("xh", "xl", "c"), 0, 0, tiled=True)
    mine = mine.reshape(2, 2, 2, block // 2, part).transpose(3, 1, 0, 2, 4)
    mine = mine.reshape(block // 2, 2 * units)
    everyone = lax.all_gather(mine, "z", axis=0, tiled=True)

    terms = lax.dot_general(
        everyone, matrices, (((1,), (1,)), ((), ())), preferred_element_type=jnp.float32
    ).astype(jnp.bfloat16)
    terms = terms.reshape(4, block, 4 * count * rows)
    arrived = lax.all_to_all(terms, "y", 0, 0, tiled=True)
    summed = jnp.sum(arrived.astype(jnp.float32), axis=0)
    summed = summed.reshape(block, 4, count, rows)
    primal = summed[:, :, 0]
    tangents = summed[:, :, 1:]
    squashed = jax.nn.sigmoid(primal)
    slope = squashed * (1.0 - squashed)
    tangent_sq = jnp.sum(tangents * tangents, axis=2)
    local_curv = jnp.sum(slope * tangent_sq, axis=(1, 2)) / (PROBES * D)

    everyones = lax.all_gather(local_curv, ("xh", "z", "c"), axis=0)
    curv = jnp.sum(everyones.reshape(2, 8, 2, block), axis=1)
    curv = curv.reshape(2, 2, 2, block // 2).transpose(2, 0, 1, 3).reshape(4 * block)

    placed = primal.astype(jnp.bfloat16).transpose(1, 0, 2)
    placed = lax.all_to_all(placed, ("xh", "c"), 0, 0, tiled=True)
    placed = placed.reshape(2, 2, 2, block // 2, rows).transpose(2, 0, 1, 3, 4)
    return (placed.reshape(4 * block, rows), curv)


def solution(mesh):
    fine = Mesh(mesh.devices.reshape(tuple(AXES.values())), tuple(AXES))
    fsdp, tp = ("xh", "z", "c"), ("xl", "y")
    return jax.shard_map(
        on_device,
        mesh=fine,
        in_specs=(
            P(fsdp, tp),
            P(),
            P(fsdp, tp),
            P(fsdp, tp),
            P(fsdp, tp),
            P(None, fsdp, tp),
        ),
        out_specs=(P(tp, fsdp), P(tp)),
        check_vma=False,
    )
```

time: 353 us -> 269 us (0.76)
  waiting for transfers between devices: 257 us -> 79 us
  blocking collectives: 37 us -> 87.2 us
  local copies, waits for them, and re-layouts: 3.53 us -> 37.9 us
  other arithmetic: 4.9 us -> 18 us
  matrix products: 22 us -> 10.5 us
  starting transfers between devices: 13.9 us -> 21.1 us
    all_gather x2, waiting for transfers between devices: 236 us -> 17.5 us  [the longest x1 17.5 us: on_device(): everyone = lax.all_gather(mine, 'z', axis=0, tiled=True)]
    ppermute x0 -> x6, waiting for transfers between devices: none -> 48.1 us  [moved(): return lax.ppermute(array, axes, [(i, (i + shift) % n) for i in range(n)])]
    all_gather x0 -> x1, blocking collectives: none -> 41.1 us  [on_device(): everyones = lax.all_gather(local_curv, ('xh', 'z', 'c'), axis=0)]
    transpose x0 -> x6, local copies, waits for them, and re-layouts: none -> 23.6 us  [the longest x1 14.1 us: on_device(): by_c.reshape(2, 2, 2, count * rows, units).transpose(1, 0, 3, 2, 4)]
    dot_general x3 -> x2, matrix products: 22 us -> 10.5 us  [the longest x1 7.51 us: on_device(): lax.dot_general(everyone, matrices, (((1,), (1,)), ((), ())), preferred_e...]
    another operation x0 -> x5, other arithmetic: none -> 10 us  [the longest x3 5.76 us: in_order_of(): jnp.stack([jnp.where(first, own, other), jnp.where(first, other, own)])]
    all_to_all x1 -> x3, blocking collectives: 37 us -> 46.1 us  [the longest x1 18.4 us: on_device(): arrived = lax.all_to_all(terms, 'y', 0, 0, tiled=True)]
    unnamed x4 -> x26, local copies, waits for them, and re-layouts: 0.01 us -> 8.3 us
  transfers between devices with their start and end apart: 4 -> 10, of which waited for: 4 -> 6; matrix products, arithmetic and copies ran while one was open for 1% -> 20% of each run, Pallas kernels for 0% -> 0%
where the time goes in v1:
time: 269 us; the launch traced here: 268 us
  blocking collectives  87.2 us (32%)
  waiting for transfers between devices  79 us (29%)
  local copies, waits for them, and re-layouts  37.9 us (14%)
  starting transfers between devices  21.1 us (8%)
  other arithmetic  18 us (7%)
  between operations  14.3 us (5%)
  matrix products  10.5 us (4%)
    ppermute x6, waiting for transfers between devices, moved(): return lax.ppermute(array, axes, [(i, (i + shift) % n) for i in range(n)])  48.1 us
    all_gather x1, blocking collectives, on_device(): everyones = lax.all_gather(local_curv, ('xh', 'z', 'c'), axis=0)  41.1 us
    all_to_all x1, blocking collectives, on_device(): arrived = lax.all_to_all(terms, 'y', 0, 0, tiled=True)  18.4 us
    all_gather x1, waiting for transfers between devices, on_device(): everyone = lax.all_gather(mine, 'z', axis=0, tiled=True)  17.5 us
    all_to_all x1, blocking collectives, on_device(): got = lax.all_to_all(sent, ('xh', 'c'), 0, 0, tiled=True)  16.6 us
    transpose x1, local copies, waits for them, and re-layouts, on_device(): by_c.reshape(2, 2, 2, count * rows, units).transpose(1, 0, 3, 2, 4)  14.1 us
    all_to_all x1, waiting for transfers between devices, on_device(): features = lax.all_to_all(spread, ('xl', 'y'), 0, 0, tiled=True)  13.4 us
    all_to_all x1, blocking collectives, on_device(): mine = lax.all_to_all(chunks, ('xh', 'xl', 'c'), 0, 0, tiled=True)  11.1 us
  transfers between devices with their start and end apart: 10, of which 6 were waited for; matrix products, arithmetic and copies ran while one was open for 20% of the time, Pallas kernels for 0%

profile of v1, /device:TPU:1, one launch (start us, length us, event | category | flops | bytes accessed | tf_op | source)
XLA Modules:
  0.0 268.0 jit_solution(2487208676732397235)
XLA Ops:
  7.2 1.2 copy.42
  8.4 1.2 copy.43
  10.1 16.6 %all_to_all.25 = bf16[4,112,640]{2,1,0:T(8,128)(2,1)} all-to-all(bf16[4,112,640]{2,1,0:T(8,128)(2,1)S(1)} %copy.44), channel_id=1, replica_groups=mesh['xh'=2,'z'=8,'c'=2,'xl'=2,'y'=4] {'xh','c'}, dimensions={0} | all-to-all | bytes 1146880 | tf_op jit(solution)/shard_map/all_to_all | solution.py:30
  26.7 1.1 broadcast_in_dim.4
  27.8 3.6 %all-to-all-start = ((bf16[8,128,448]{1,2,0:T(8,128)(2,1)}), bf16[8,128,448]{1,2,0:T(8,128)(2,1)S(1)}, u32[]{:S(2)}, u32[]{:S(2)}) async-start(bf16[8,128,448]{1,2,0:T(8,128)(2,1)} %broadcast_in_dim.4), calls=%async_computation | async-start | bytes 1835008 | tf_op jit(solution)/shard_map/all_to_all | solution.py:37
  31.5 13.4 %all-to-all-done = bf16[8,128,448]{1,2,0:T(8,128)(2,1)S(1)} async-done(((bf16[8,128,448]{1,2,0:T(8,128)(2,1)}), bf16[8,128,448]{1,2,0:T(8,128)(2,1)S(1)}, u32[]{:S(2)}, u32[]{:S(2)}) %all-to-all-start) | async-done | bytes 917536 | tf_op jit(solution)/shard_map/all_to_all | solution.py:37
  46.5 1.0 pad_maximum_fusion.3
  47.6 3.3 %collective-permute-start.4 = (bf16[336,1280]{1,0:T(8,128)(2,1)}, bf16[336,1280]{1,0:T(8,128)(2,1)}, u32[]{:S(2)}, u32[]{:S(2)}) collective-permute-start(bf16[336,1280]{1,0:T(8,128)(2,1)} %bitcast.22), channel_id=1, source_target_pairs={{0,132},{4,0},{128,4},{132,128},{1,133},{5,1},{129,5},{133,129},{2... | collective-permute-start | bytes 2580488 | tf_op jit(solution)/shard_map/ppermute | solution.py:16
  51.4 17.2 %collective-permute-done = bf16[128,3584]{0,1:T(8,128)(2,1)} collective-permute-done((bf16[128,3584]{0,1:T(8,128)(2,1)S(1)}, bf16[128,3584]{0,1:T(8,128)(2,1)}, u32[]{:S(2)}, u32[]{:S(2)}) %collective-permute-start) | collective-permute-done | bytes 917536 | tf_op jit(solution)/shard_map/ppermute | solution.py:16
  68.6 2.6 select_bitcast_fusion.3
  71.2 1.4 pad_maximum_fusion.2
  72.6 3.2 %collective-permute-start.1 = (bf16[2,128,3584]{1,2,0:T(8,128)(2,1)}, bf16[2,128,3584]{1,2,0:T(8,128)(2,1)}, u32[]{:S(2)}, u32[]{:S(2)}) collective-permute-start(bf16[2,128,3584]{1,2,0:T(8,128)(2,1)} %pad_maximum_fusion.2), channel_id=1, source_target_pairs={{0,8},{8,0},{1,9},{9,1},{2,10},{10,2},{3,11},{11,3},{4,12},{12,4},... | collective-permute-start | bytes 5505032 | tf_op jit(solution)/shard_map/ppermute | solution.py:16
  75.9 10.4 %collective-permute-done.4 = bf16[336,1280]{1,0:T(8,128)(2,1)} collective-permute-done((bf16[336,1280]{1,0:T(8,128)(2,1)}, bf16[336,1280]{1,0:T(8,128)(2,1)}, u32[]{:S(2)}, u32[]{:S(2)}) %collective-permute-start.4) | collective-permute-done | bytes 860192 | tf_op jit(solution)/shard_map/ppermute | solution.py:16
  87.0 19.7 %collective-permute-done.2 = bf16[336,1280]{1,0:T(8,128)(2,1)} collective-permute-done((bf16[336,1280]{1,0:T(8,128)(2,1)}, bf16[336,1280]{1,0:T(8,128)(2,1)}, u32[]{:S(2)}, u32[]{:S(2)}) %collective-permute-start.2) | collective-permute-done | bytes 860192 | tf_op jit(solution)/shard_map/ppermute | solution.py:16
  106.7 2.1 pad_maximum_fusion
  109.1 2.1 pad_maximum_fusion.1
  112.1 1.7 select_bitcast_fusion.1
  113.9 2.1 maximum_bitcast_fusion.1
  116.0 6.0 %copy.41 = bf16[2,2,128,3584]{3,2,1,0:T(8,128)(2,1)} copy(bf16[2,2,128,3584]{2,3,0,1:T(8,128)(2,1)} %maximum_bitcast_fusion.1) | data formatting | bytes 7340032 | tf_op jit(solution)/shard_map/transpose | solution.py:44
  122.0 2.8 %copy.45 = bf16[2,8,2,112,640]{4,3,2,1,0:T(8,128)(2,1)S(1)} copy(bf16[2,8,2,112,640]{4,3,2,0,1:T(8,128)(2,1)} %bitcast.81) | data formatting | bytes 9175040 | tf_op jit(solution)/shard_map/transpose | solution.py:32
  125.4 3.0 %fusion.8 = f32[512,640]{1,0:T(8,128)S(1)} fusion(bf16[512,3584]{1,0:T(8,128)(2,1)S(1)} %bitcast.83, bf16[3584,640]{1,0:T(8,128)(2,1)S(1)} %bitcast.82), kind=kOutput, calls=%fused_computation.37 | convolution fusion | flops 2348810240 | bytes 9568256 | tf_op jit(solution)/shard_map/dot_general | solution.py:46
  128.8 11.1 %all_to_all.26 = bf16[8,64,320]{2,1,0:T(8,128)(2,1)S(1)} all-to-all(bf16[8,64,320]{2,1,0:T(8,128)(2,1)S(1)} %bitcast.87), channel_id=1, replica_groups=mesh['xh'=2,'z'=8,'c'=2,'xl'=2,'y'=4] {'xh','xl','c'}, dimensions={0} | all-to-all | bytes 655360 | tf_op jit(solution)/shard_map/all_to_all | solution.py:64
  139.9 1.2 copy.59
  141.1 2.0 reshape.100
  143.2 2.4 broadcast_select_fusion.1
  146.2 14.1 %copy.48 = bf16[2,2,336,2,1280]{4,3,2,1,0:T(2,128)(2,1)S(1)} copy(bf16[2,2,336,2,1280]{4,2,3,0,1:T(8,128)(2,1)S(1)} %maximum_bitcast_fusion) | data formatting | bytes 13762560 | tf_op jit(solution)/shard_map/transpose | solution.py:59
  160.3 4.2 %copy.55 = bf16[168,8,2,1280]{3,1,2,0:T(8,128)(2,1)} copy(bf16[168,8,2,1280]{3,2,1,0:T(2,128)(2,1)S(1)} %bitcast.76) | data formatting | bytes 13762560
  164.5 17.5 %all-gather.6.cloned.1.call-done = bf16[512,2560]{1,0:T(8,128)(2,1)} async-done(((bf16[64,2560]{1,0:T(8,128)(2,1)}), bf16[512,2560]{1,0:T(8,128)(2,1)}) %all-gather.6.cloned.1.call-update) | async-done | bytes 2621456 | tf_op jit(solution)/shard_map/all_gather | solution.py:67
  182.0 7.5 %fusion.2 = bf16[168,4,8,128]{3,2,1,0:T(8,128)(2,1)S(1)} fusion(bf16[512,2560]{1,0:T(8,128)(2,1)} %all-gather.6.cloned.1.call-done, bf16[1344,2560]{1,0:T(8,128)(2,1)} %bitcast.79), kind=kOutput, calls=%fused_computation.15 | convolution fusion | flops 3523903488 | bytes 10878976 | tf_op jit(solution)/shard_map/dot_general | solution.py:69
  189.8 18.4 %all_to_all.27 = bf16[4,128,1344]{1,2,0:T(8,128)(2,1)S(1)} all-to-all(bf16[4,128,1344]{1,2,0:T(8,128)(2,1)S(1)} %bitcast.80), channel_id=1, replica_groups=mesh['xh'=2,'z'=8,'c'=2,'xl'=2,'y'=4] {'y'}, dimensions={0} | all-to-all | bytes 2752512 | tf_op jit(solution)/shard_map/all_to_all | solution.py:73
  209.1 9.2 %all-to-all-start.4 = ((bf16[4,128,112]{1,2,0:T(8,128)(2,1)}), bf16[4,128,112]{1,2,0:T(8,128)(2,1)S(1)}, u32[]{:S(2)}, u32[]{:S(2)}) async-start(bf16[4,128,112]{1,2,0:T(8,128)(2,1)} %fusion.7), calls=%async_computation.4 | async-start | bytes 229376 | tf_op jit(solution)/shard_map/all_to_all | solution.py:88
  218.4 41.1 %all-gather.2 = f32[32,1,128]{2,1,0:T(1,128)S(1)} all-gather(f32[1,1,128]{2,1,0:T(1,128)S(1)} %multiply_bitcast_fusion), channel_id=3, replica_groups=mesh['xh'=2,'z'=8,'c'=2,'xl'=2,'y'=4] {'xh','z','c'}, dimensions={0}, use_global_device_ids=true | all-gather | bytes 16896 | tf_op jit(solution)/shard_map/all_gather | solution.py:83
  (58 shorter events, 9.2 us)
Async XLA Ops:
  7.2 19.5 %copy-start.9 = (bf16[128,448]{0,1:T(8,128)(2,1)S(1)}, bf16[128,448]{0,1:T(8,128)(2,1)}, u32[]{:S(2)}) copy-start(bf16[128,448]{0,1:T(8,128)(2,1)} %param.6) | copy-start | bytes 344068
  7.2 114.8 %all-gather.8.cloned.1.call-start = ((), (), s32[]{:S(2)}) async-start(), calls=%async_computation.6 | async-start | bytes 5160960 | tf_op jit(solution)/shard_map/all_gather | solution.py:31
  9.6 21.9 %copy-start.10 = (bf16[3584]{0:T(1024)(128)(2,1)S(1)}, bf16[3584]{0:T(1024)(128)(2,1)}, u32[]{:S(2)}) copy-start(bf16[3584]{0:T(1024)(128)(2,1)} %param.7) | copy-start | bytes 21508
  10.0 36.5 %copy-start.7 = (bf16[2,112,1280]{2,1,0:T(8,128)(2,1)S(1)}, bf16[2,112,1280]{2,1,0:T(8,128)(2,1)}, u32[]{:S(2)}) copy-start(bf16[2,112,1280]{2,1,0:T(8,128)(2,1)} %param.11) | copy-start | bytes 1720324
  10.0 36.5 %copy-start.8 = (bf16[112,1280]{1,0:T(8,128)(2,1)S(1)}, bf16[112,1280]{1,0:T(8,128)(2,1)}, u32[]{:S(2)}) copy-start(bf16[112,1280]{1,0:T(8,128)(2,1)} %param.10) | copy-start | bytes 860164
  27.8 17.0 %all-to-all-start = ((bf16[8,128,448]{1,2,0:T(8,128)(2,1)}), bf16[8,128,448]{1,2,0:T(8,128)(2,1)S(1)}, u32[]{:S(2)}, u32[]{:S(2)}) async-start(bf16[8,128,448]{1,2,0:T(8,128)(2,1)} %broadcast_in_dim.4), calls=%async_computation | async-start | bytes 1835008 | tf_op jit(solution)/shard_map/all_to_all | solution.py:37
  31.4 150.6 %all-gather.6.cloned.1.call-start = ((), (), s32[]{:S(2)}) async-start(), calls=%async_computation.5 | async-start | bytes 2949120 | tf_op jit(solution)/shard_map/all_gather | solution.py:67
  45.9 22.7 %collective-permute-start = (bf16[128,3584]{0,1:T(8,128)(2,1)S(1)}, bf16[128,3584]{0,1:T(8,128)(2,1)}, u32[]{:S(2)}, u32[]{:S(2)}) collective-permute-start(bf16[128,3584]{0,1:T(8,128)(2,1)S(1)} %fusion.1), channel_id=1, source_target_pairs={{0,128},{128,0},{1,129},{129,1},{2,130},{130,2},{3,131},{131,3},{4... | collective-permute-start | bytes 2752520 | tf_op jit(solution)/shard_map/ppermute | solution.py:16
  47.6 38.7 %collective-permute-start.4 = (bf16[336,1280]{1,0:T(8,128)(2,1)}, bf16[336,1280]{1,0:T(8,128)(2,1)}, u32[]{:S(2)}, u32[]{:S(2)}) collective-permute-start(bf16[336,1280]{1,0:T(8,128)(2,1)} %bitcast.22), channel_id=1, source_target_pairs={{0,132},{4,0},{128,4},{132,128},{1,133},{5,1},{129,5},{133,129},{2... | collective-permute-start | bytes 2580488 | tf_op jit(solution)/shard_map/ppermute | solution.py:16
  50.8 36.2 %collective-permute-start.3 = (bf16[336,1280]{1,0:T(8,128)(2,1)}, bf16[336,1280]{1,0:T(8,128)(2,1)}, u32[]{:S(2)}, u32[]{:S(2)}) collective-permute-start(bf16[336,1280]{1,0:T(8,128)(2,1)} %bitcast.22), channel_id=1, source_target_pairs={{0,128},{4,132},{128,0},{132,4},{1,129},{5,133},{129,1},{133,5},{2... | collective-permute-start | bytes 2580488 | tf_op jit(solution)/shard_map/ppermute | solution.py:16
  50.8 55.9 %collective-permute-start.2 = (bf16[336,1280]{1,0:T(8,128)(2,1)}, bf16[336,1280]{1,0:T(8,128)(2,1)}, u32[]{:S(2)}, u32[]{:S(2)}) collective-permute-start(bf16[336,1280]{1,0:T(8,128)(2,1)} %bitcast.22), channel_id=1, source_target_pairs={{0,4},{4,128},{128,132},{132,0},{1,5},{5,129},{129,133},{133,1},{2... | collective-permute-start | bytes 2580488 | tf_op jit(solution)/shard_map/ppermute | solution.py:16
  72.6 39.5 %collective-permute-start.1 = (bf16[2,128,3584]{1,2,0:T(8,128)(2,1)}, bf16[2,128,3584]{1,2,0:T(8,128)(2,1)}, u32[]{:S(2)}, u32[]{:S(2)}) collective-permute-start(bf16[2,128,3584]{1,2,0:T(8,128)(2,1)} %pad_maximum_fusion.2), channel_id=1, source_target_pairs={{0,8},{8,0},{1,9},{9,1},{2,10},{10,2},{3,11},{11,3},{4,12},{12,4},... | collective-permute-start | bytes 5505032 | tf_op jit(solution)/shard_map/ppermute | solution.py:16
  109.1 2.2 copy-start
  109.1 2.2 copy-start.2
  109.1 2.5 copy-start.4
  111.6 31.5 %collective-permute-start.5 = (bf16[4,336,1280]{2,1,0:T(8,128)(2,1)}, bf16[4,336,1280]{2,1,0:T(8,128)(2,1)}, u32[]{:S(2)}, u32[]{:S(2)}) collective-permute-start(bf16[4,336,1280]{2,1,0:T(8,128)(2,1)} %pad_maximum_fusion.1), channel_id=1, source_target_pairs={{0,8},{8,0},{1,9},{9,1},{2,10},{10,2},{3,11},{11,3},{4,12},{12,4},... | collective-permute-start | bytes 10321928 | tf_op jit(solution)/shard_map/ppermute | solution.py:16
  122.0 3.4 %copy-start.6 = (bf16[2,2,128,3584]{3,2,1,0:T(8,128)(2,1)S(1)}, bf16[2,2,128,3584]{3,2,1,0:T(8,128)(2,1)}, u32[]{:S(2)}) copy-start(bf16[2,2,128,3584]{3,2,1,0:T(8,128)(2,1)} %copy.41) | copy-start | bytes 11010052
  128.4 14.7 %copy-start.1 = (bf16[1,336,1280]{2,1,0:T(8,128)(2,1)S(1)}, bf16[1,336,1280]{2,1,0:T(8,128)(2,1)}, u32[]{:S(2)}) copy-start(bf16[1,336,1280]{2,1,0:T(8,128)(2,1)} %copy-done) | copy-start | bytes 2580484
  128.4 14.7 %copy-start.3 = (bf16[1,336,1280]{2,1,0:T(8,128)(2,1)S(1)}, bf16[1,336,1280]{2,1,0:T(8,128)(2,1)}, u32[]{:S(2)}) copy-start(bf16[1,336,1280]{2,1,0:T(8,128)(2,1)} %copy-done.2) | copy-start | bytes 2580484
  128.4 14.7 %copy-start.5 = (bf16[1,336,1280]{2,1,0:T(8,128)(2,1)S(1)}, bf16[1,336,1280]{2,1,0:T(8,128)(2,1)}, u32[]{:S(2)}) copy-start(bf16[1,336,1280]{2,1,0:T(8,128)(2,1)} %copy-done.4) | copy-start | bytes 2580484
  209.1 51.2 %all-to-all-start.4 = ((bf16[4,128,112]{1,2,0:T(8,128)(2,1)}), bf16[4,128,112]{1,2,0:T(8,128)(2,1)S(1)}, u32[]{:S(2)}, u32[]{:S(2)}) async-start(bf16[4,128,112]{1,2,0:T(8,128)(2,1)} %fusion.7), calls=%async_computation.4 | async-start | bytes 229376 | tf_op jit(solution)/shard_map/all_to_all | solution.py:88
Sparse Core Ops, SparseCore 0:
  26.8 58.1 all-gather.7
  143.3 38.6 all-gather.5
